TPU v7x, 256 devices: a whole 4x4x8 slice. The times are simulated.
256 devices in a mesh: node: 32 (over y, x, core), head: 8 (over z).
Axes of the slice: x: 4, y: 4, z: 8, core: 2. Of those that a mesh axis runs over, the one named last changes fastest.
Arguments:
- features: bfloat16 [65536, 100], P('node'), may hold values from -6 to 6
- proj_weight: bfloat16 [100, 512], P(None, 'head'), may hold values from -0.625 to 0.625
- score_src: float32 [8, 64], P('head'), may hold values from -150 to 150
- score_dst: float32 [8, 64], P('head'), may hold values from -0.75 to 0.75
- request_rows: int32 [32, 32, 256], P('node'), may hold values from 0 to 2047
- slot_index: int32 [16384, 16], P('node'), may hold values from 0 to 8191
- slot_count: int32 [16384], P('node'), may hold values from 1 to 16
- out_weight: bfloat16 [512, 512], replicated, may hold values from -0.25 to 0.25
Outputs:
- layer_out: bfloat16 [16384, 512], P(('node', 'head'))
All inputs are finite; a program needn't handle non-finite values.
Results may differ from a plain program's by a relative error of at most 0.012.
The roundings to bfloat16 on the way count: a program that leaves them out, or rounds other values in their place, can miss the bound.
Values may be sent and summed in bfloat16 or wider, within the bound.
A program may use at most 64 MiB of HBM per device.

v0:
```python
import math

import jax
import jax.numpy as jnp
from jax import lax
from jax.sharding import PartitionSpec as P


def pick_rows(table, row_index):
    total = row_index.shape[0]
    block_rows = math.gcd(total, 1024)
    columns = lax.iota(jnp.int32, table.shape[0])

    def select_block(row_ids):
        hot_table = (row_ids[:, None] == columns[None, :]).astype(table.dtype)
        return jnp.dot(hot_table, table, preferred_element_type=jnp.float32).astype(table.dtype)

    chosen = lax.map(select_block, row_index.reshape(total // block_rows, block_rows))
    return chosen.reshape(total, table.shape[1])


def local(
    features, proj_weight, score_src, score_dst, request_rows, slot_index, slot_count, out_weight
):
    groups = lax.axis_size("node")
    capacity = request_rows.shape[2]
    width = proj_weight.shape[1]
    local_heads = score_src.shape[0]
    head_dim = score_src.shape[1]
    dst_rows = slot_index.shape[0]
    slot_total = slot_index.shape[1]
    wanted = lax.all_to_all(request_rows, "node", split_axis=1, concat_axis=0, tiled=True).reshape(
        groups * capacity
    )
    picked = pick_rows(features, wanted)
    owned = jnp.dot(picked, proj_weight, preferred_element_type=jnp.float32).astype(jnp.bfloat16)
    fetched = lax.all_to_all(
        owned.reshape(groups, capacity, width), "node", split_axis=0, concat_axis=0, tiled=True
    )
    buffer_rows = fetched.reshape(groups * capacity, width)
    zvals = pick_rows(buffer_rows, slot_index.reshape(-1)).reshape(
        dst_rows, slot_total, local_heads, head_dim
    )
    src_part = jnp.einsum("rshd,hd->rsh", zvals.astype(jnp.float32), score_src)
    dst_part = jnp.einsum("rhd,hd->rh", zvals[:, 0].astype(jnp.float32), score_dst)
    logit = src_part + dst_part[:, None, :]
    logit = jnp.where(logit > 0, logit, 0.2 * logit)
    live_mask = (jnp.arange(slot_total, dtype=jnp.int32)[None, :] < slot_count[:, None])[:, :, None]
    logit = jnp.where(live_mask, logit, -1e30)
    peak = jnp.max(logit, axis=1, keepdims=True)
    weights = jnp.where(live_mask, jnp.exp(logit - peak), 0.0)
    alpha = (weights / jnp.sum(weights, axis=1, keepdims=True)).astype(jnp.bfloat16)
    summed = jnp.einsum("rsh,rshd->rhd", alpha, zvals, preferred_element_type=jnp.float32)
    hidden = jax.nn.elu(summed).astype(jnp.bfloat16).reshape(dst_rows, local_heads * head_dim)
    gathered = lax.all_to_all(hidden, "head", split_axis=0, concat_axis=1, tiled=True)
    layer_out = jnp.dot(gathered, out_weight, preferred_element_type=jnp.float32).astype(
        jnp.bfloat16
    )
    return layer_out


def solution(mesh):
    in_specs = (
        P("node", None),
        P(None, "head"),
        P("head", None),
        P("head", None),
        P("node", None, None),
        P("node", None),
        P("node"),
        P(),
    )
    out_specs = P(("node", "head"), None)
    return jax.shard_map(local, mesh=mesh, in_specs=in_specs, out_specs=out_specs, check_vma=False)
```

profile of v0, /device:TPU:1, one launch (start us, length us, event | category | flops | bytes accessed | tf_op | source)
XLA Modules:
  0.0 161.8 jit_solution(8266049617888468764)
XLA Ops:
  0.0 1.5 copy.45
  1.5 8.6 %all-to-all-start = ((s32[1,32,256]{2,0,1:T(1,128)}), s32[1,32,256]{2,0,1:T(1,128)S(1)}, u32[]{:S(2)}, u32[]{:S(2)}) async-start(s32[1,32,256]{2,0,1:T(1,128)} %copy.45), calls=%async_computation | async-start | bytes 65536 | tf_op jit(solution)/shard_map/all_to_all | solution.py:32
  10.1 7.2 %all-to-all-done = s32[1,32,256]{2,0,1:T(1,128)S(1)} async-done(((s32[1,32,256]{2,0,1:T(1,128)}), s32[1,32,256]{2,0,1:T(1,128)S(1)}, u32[]{:S(2)}, u32[]{:S(2)}) %all-to-all-start) | async-done | bytes 32800 | tf_op jit(solution)/shard_map/all_to_all | solution.py:32
  17.3 0.1 reduce.6
  17.4 23.2 %while.22 = (s32[]{:T(128)}, bf16[8,1024,100]{1,2,0:T(8,128)(2,1)S(1)}, s32[8,1024]{1,0:T(8,128)S(1)}, bf16[2048,100]{0,1:T(8,128)(2,1)}, s32[]{:T(128)}) while((s32[]{:T(128)}, bf16[8,1024,100]{1,2,0:T(8,128)(2,1)S(1)}, s32[8,1024]{1,0:T(8,128)S(1)}, bf16[2048,100]{0,1:T(8,128)(2,1)}, s32[]{:T(128)}) %tuple.39), condition=%wide.region_1.2_spmd.clone, body=%wide.region_0.1_spmd.clone.sunk | while | flops 421629952 | bytes 634949 | solution.py:18
  17.4 2.9 %fusion.39 = bf16[8,1024,100]{1,2,0:T(8,128)(2,1)S(1)} fusion(bf16[8,1024,100]{1,2,0:T(8,128)(2,1)S(1)} %get-tuple-element.161, s32[]{:T(128)} %get-tuple-element.160, bf16[2048,100]{0,1:T(8,128)(2,1)} %get-tuple-element.168, s32[1024]{0:T(1024)S(1)} %bitcast.81), kind=kOutput, calls=%fused_computation.7.clone.1 | convolution fusion | flops 421629952 | bytes 626692 | tf_op jit(solution)/shard_map/while/body/eval_jaxpr/dot_general | solution.py:16
  20.3 2.9 %fusion.39 = bf16[8,1024,100]{1,2,0:T(8,128)(2,1)S(1)} fusion(bf16[8,1024,100]{1,2,0:T(8,128)(2,1)S(1)} %get-tuple-element.161, s32[]{:T(128)} %get-tuple-element.160, bf16[2048,100]{0,1:T(8,128)(2,1)} %get-tuple-element.168, s32[1024]{0:T(1024)S(1)} %bitcast.81), kind=kOutput, calls=%fused_computation.7.clone.1 | convolution fusion | flops 421629952 | bytes 626692 | tf_op jit(solution)/shard_map/while/body/eval_jaxpr/dot_general | solution.py:16
  23.2 2.9 %fusion.39 = bf16[8,1024,100]{1,2,0:T(8,128)(2,1)S(1)} fusion(bf16[8,1024,100]{1,2,0:T(8,128)(2,1)S(1)} %get-tuple-element.161, s32[]{:T(128)} %get-tuple-element.160, bf16[2048,100]{0,1:T(8,128)(2,1)} %get-tuple-element.168, s32[1024]{0:T(1024)S(1)} %bitcast.81), kind=kOutput, calls=%fused_computation.7.clone.1 | convolution fusion | flops 421629952 | bytes 626692 | tf_op jit(solution)/shard_map/while/body/eval_jaxpr/dot_general | solution.py:16
  26.1 2.9 %fusion.39 = bf16[8,1024,100]{1,2,0:T(8,128)(2,1)S(1)} fusion(bf16[8,1024,100]{1,2,0:T(8,128)(2,1)S(1)} %get-tuple-element.161, s32[]{:T(128)} %get-tuple-element.160, bf16[2048,100]{0,1:T(8,128)(2,1)} %get-tuple-element.168, s32[1024]{0:T(1024)S(1)} %bitcast.81), kind=kOutput, calls=%fused_computation.7.clone.1 | convolution fusion | flops 421629952 | bytes 626692 | tf_op jit(solution)/shard_map/while/body/eval_jaxpr/dot_general | solution.py:16
  29.1 2.9 %fusion.39 = bf16[8,1024,100]{1,2,0:T(8,128)(2,1)S(1)} fusion(bf16[8,1024,100]{1,2,0:T(8,128)(2,1)S(1)} %get-tuple-element.161, s32[]{:T(128)} %get-tuple-element.160, bf16[2048,100]{0,1:T(8,128)(2,1)} %get-tuple-element.168, s32[1024]{0:T(1024)S(1)} %bitcast.81), kind=kOutput, calls=%fused_computation.7.clone.1 | convolution fusion | flops 421629952 | bytes 626692 | tf_op jit(solution)/shard_map/while/body/eval_jaxpr/dot_general | solution.py:16
  32.0 2.9 %fusion.39 = bf16[8,1024,100]{1,2,0:T(8,128)(2,1)S(1)} fusion(bf16[8,1024,100]{1,2,0:T(8,128)(2,1)S(1)} %get-tuple-element.161, s32[]{:T(128)} %get-tuple-element.160, bf16[2048,100]{0,1:T(8,128)(2,1)} %get-tuple-element.168, s32[1024]{0:T(1024)S(1)} %bitcast.81), kind=kOutput, calls=%fused_computation.7.clone.1 | convolution fusion | flops 421629952 | bytes 626692 | tf_op jit(solution)/shard_map/while/body/eval_jaxpr/dot_general | solution.py:16
  34.9 2.9 %fusion.39 = bf16[8,1024,100]{1,2,0:T(8,128)(2,1)S(1)} fusion(bf16[8,1024,100]{1,2,0:T(8,128)(2,1)S(1)} %get-tuple-element.161, s32[]{:T(128)} %get-tuple-element.160, bf16[2048,100]{0,1:T(8,128)(2,1)} %get-tuple-element.168, s32[1024]{0:T(1024)S(1)} %bitcast.81), kind=kOutput, calls=%fused_computation.7.clone.1 | convolution fusion | flops 421629952 | bytes 626692 | tf_op jit(solution)/shard_map/while/body/eval_jaxpr/dot_general | solution.py:16
  37.8 2.9 %fusion.39 = bf16[8,1024,100]{1,2,0:T(8,128)(2,1)S(1)} fusion(bf16[8,1024,100]{1,2,0:T(8,128)(2,1)S(1)} %get-tuple-element.161, s32[]{:T(128)} %get-tuple-element.160, bf16[2048,100]{0,1:T(8,128)(2,1)} %get-tuple-element.168, s32[1024]{0:T(1024)S(1)} %bitcast.81), kind=kOutput, calls=%fused_computation.7.clone.1 | convolution fusion | flops 421629952 | bytes 626692 | tf_op jit(solution)/shard_map/while/body/eval_jaxpr/dot_general | solution.py:16
  40.6 0.9 copy.73
  41.6 0.1 pad
  41.7 0.0 copy-start.3
  41.7 1.1 copy.69
  42.8 0.4 convolution_convert_fusion
  43.3 1.1 copy.74
  44.4 4.0 %all-to-all-start.1 = ((bf16[32,256,64]{1,2,0:T(8,128)(2,1)}), bf16[32,256,64]{1,2,0:T(8,128)(2,1)S(1)}, u32[]{:S(2)}, u32[]{:S(2)}) async-start(bf16[32,256,64]{1,2,0:T(8,128)(2,1)} %bitcast.57), calls=%async_computation.1 | async-start | bytes 2097152 | tf_op jit(solution)/shard_map/all_to_all | solution.py:37
  48.4 0.1 copy.44
  48.5 0.2 reshape_reshape.9
  48.7 16.8 %all-to-all-done.1 = bf16[32,256,64]{1,2,0:T(8,128)(2,1)S(1)} async-done(((bf16[32,256,64]{1,2,0:T(8,128)(2,1)}), bf16[32,256,64]{1,2,0:T(8,128)(2,1)S(1)}, u32[]{:S(2)}, u32[]{:S(2)}) %all-to-all-start.1) | async-done | bytes 1048608 | tf_op jit(solution)/shard_map/all_to_all | solution.py:37
  65.5 1.8 %copy.64 = bf16[32,256,64]{2,1,0:T(8,128)(2,1)} copy(bf16[32,256,64]{1,2,0:T(8,128)(2,1)S(1)} %all-to-all-done.1) | data formatting | bytes 2097152
  67.3 70.9 %while.23 = (s32[]{:T(128)}, bf16[8,1024,64]{1,2,0:T(8,128)(2,1)}, s32[8,1024]{1,0:T(8,128)S(1)}, bf16[8192,64]{1,0:T(8,128)(2,1)}, s32[]{:T(128)}) while((s32[]{:T(128)}, bf16[8,1024,64]{1,2,0:T(8,128)(2,1)}, s32[8,1024]{1,0:T(8,128)S(1)}, bf16[8192,64]{1,0:T(8,128)(2,1)}, s32[]{:T(128)}) %tuple.45), condition=%wide.region_3.4_spmd.clone, body=%wide.region_2.3_spmd.clone.sunk | while | flops 1082195968 | bytes 2241089 | solution.py:18
  67.4 8.9 %fusion.41 = bf16[8,1024,64]{1,2,0:T(8,128)(2,1)} fusion(bf16[8,1024,64]{1,2,0:T(8,128)(2,1)} %get-tuple-element.176, s32[]{:T(128)} %get-tuple-element.175, bf16[8192,64]{1,0:T(8,128)(2,1)} %get-tuple-element.183, s32[1024]{0:T(1024)S(1)} %bitcast.82), kind=kOutput, calls=%fused_computation.14.clone.1 | convolution fusion | flops 1082195968 | bytes 2232832 | tf_op jit(solution)/shard_map/while/body/eval_jaxpr/dot_general | solution.py:16
  76.2 8.8 %fusion.41 = bf16[8,1024,64]{1,2,0:T(8,128)(2,1)} fusion(bf16[8,1024,64]{1,2,0:T(8,128)(2,1)} %get-tuple-element.176, s32[]{:T(128)} %get-tuple-element.175, bf16[8192,64]{1,0:T(8,128)(2,1)} %get-tuple-element.183, s32[1024]{0:T(1024)S(1)} %bitcast.82), kind=kOutput, calls=%fused_computation.14.clone.1 | convolution fusion | flops 1082195968 | bytes 2232832 | tf_op jit(solution)/shard_map/while/body/eval_jaxpr/dot_general | solution.py:16
  85.1 8.8 %fusion.41 = bf16[8,1024,64]{1,2,0:T(8,128)(2,1)} fusion(bf16[8,1024,64]{1,2,0:T(8,128)(2,1)} %get-tuple-element.176, s32[]{:T(128)} %get-tuple-element.175, bf16[8192,64]{1,0:T(8,128)(2,1)} %get-tuple-element.183, s32[1024]{0:T(1024)S(1)} %bitcast.82), kind=kOutput, calls=%fused_computation.14.clone.1 | convolution fusion | flops 1082195968 | bytes 2232832 | tf_op jit(solution)/shard_map/while/body/eval_jaxpr/dot_general | solution.py:16
  93.9 8.9 %fusion.41 = bf16[8,1024,64]{1,2,0:T(8,128)(2,1)} fusion(bf16[8,1024,64]{1,2,0:T(8,128)(2,1)} %get-tuple-element.176, s32[]{:T(128)} %get-tuple-element.175, bf16[8192,64]{1,0:T(8,128)(2,1)} %get-tuple-element.183, s32[1024]{0:T(1024)S(1)} %bitcast.82), kind=kOutput, calls=%fused_computation.14.clone.1 | convolution fusion | flops 1082195968 | bytes 2232832 | tf_op jit(solution)/shard_map/while/body/eval_jaxpr/dot_general | solution.py:16
  102.8 8.8 %fusion.41 = bf16[8,1024,64]{1,2,0:T(8,128)(2,1)} fusion(bf16[8,1024,64]{1,2,0:T(8,128)(2,1)} %get-tuple-element.176, s32[]{:T(128)} %get-tuple-element.175, bf16[8192,64]{1,0:T(8,128)(2,1)} %get-tuple-element.183, s32[1024]{0:T(1024)S(1)} %bitcast.82), kind=kOutput, calls=%fused_computation.14.clone.1 | convolution fusion | flops 1082195968 | bytes 2232832 | tf_op jit(solution)/shard_map/while/body/eval_jaxpr/dot_general | solution.py:16
  111.7 8.9 %fusion.41 = bf16[8,1024,64]{1,2,0:T(8,128)(2,1)} fusion(bf16[8,1024,64]{1,2,0:T(8,128)(2,1)} %get-tuple-element.176, s32[]{:T(128)} %get-tuple-element.175, bf16[8192,64]{1,0:T(8,128)(2,1)} %get-tuple-element.183, s32[1024]{0:T(1024)S(1)} %bitcast.82), kind=kOutput, calls=%fused_computation.14.clone.1 | convolution fusion | flops 1082195968 | bytes 2232832 | tf_op jit(solution)/shard_map/while/body/eval_jaxpr/dot_general | solution.py:16
  120.5 8.8 %fusion.41 = bf16[8,1024,64]{1,2,0:T(8,128)(2,1)} fusion(bf16[8,1024,64]{1,2,0:T(8,128)(2,1)} %get-tuple-element.176, s32[]{:T(128)} %get-tuple-element.175, bf16[8192,64]{1,0:T(8,128)(2,1)} %get-tuple-element.183, s32[1024]{0:T(1024)S(1)} %bitcast.82), kind=kOutput, calls=%fused_computation.14.clone.1 | convolution fusion | flops 1082195968 | bytes 2232832 | tf_op jit(solution)/shard_map/while/body/eval_jaxpr/dot_general | solution.py:16
  129.4 8.9 %fusion.41 = bf16[8,1024,64]{1,2,0:T(8,128)(2,1)} fusion(bf16[8,1024,64]{1,2,0:T(8,128)(2,1)} %get-tuple-element.176, s32[]{:T(128)} %get-tuple-element.175, bf16[8192,64]{1,0:T(8,128)(2,1)} %get-tuple-element.183, s32[1024]{0:T(1024)S(1)} %bitcast.82), kind=kOutput, calls=%fused_computation.14.clone.1 | convolution fusion | flops 1082195968 | bytes 2232832 | tf_op jit(solution)/shard_map/while/body/eval_jaxpr/dot_general | solution.py:16
  138.3 2.0 %copy.50 = bf16[8,1024,64]{2,1,0:T(8,128)(2,1)S(1)} copy(bf16[8,1024,64]{1,2,0:T(8,128)(2,1)} %get-tuple-element.60) | data formatting | bytes 2097152 | tf_op jit(solution)/shard_map/while | solution.py:18
  140.3 0.1 slice.4
  140.5 0.1 copy.52
  140.6 1.2 multiply_reduce_fusion.1
  141.8 0.1 copy.59
  141.9 0.1 fusion.16
  142.1 0.1 copy.67
  142.2 2.9 %multiply_reduce_fusion = f32[512,64]{1,0:T(8,128)S(1)} fusion(bf16[512,16,64]{2,1,0:T(8,128)(2,1)S(1)} %bitcast.73, f32[512,16]{1,0:T(8,128)S(1)} %copy.67), kind=kLoop, calls=%fused_computation.17 | loop fusion | flops 1540096 | bytes 1212416
  145.1 0.1 copy.63
  145.2 0.1 fusion.15
  145.3 0.1 all_to_all.26
  145.5 0.2 reshape.91
  145.6 15.2 %all_to_all.33 = bf16[8,2,2048]{2,1,0:T(2,128)(2,1)S(1)} all-to-all(bf16[8,2,2048]{2,1,0:T(2,128)(2,1)S(1)} %reshape.91), channel_id=1, replica_groups=mesh['node'=32,'head'=8] {'head'}, dimensions={0} | all-to-all | bytes 131072 | tf_op jit(solution)/shard_map/all_to_all | solution.py:55
  160.8 0.1 reshape.92
  161.0 0.9 convolution_convert_fusion.1
  (34 shorter events, 0.3 us)
Async XLA Ops:
  0.0 161.0 %copy-start = (bf16[512,512]{1,0:T(8,128)(2,1)S(1)}, bf16[512,512]{1,0:T(8,128)(2,1)}, u32[]{:S(2)}) copy-start(bf16[512,512]{1,0:T(8,128)(2,1)} %param.19) | copy-start | bytes 1572868
  1.5 15.8 %all-to-all-start = ((s32[1,32,256]{2,0,1:T(1,128)}), s32[1,32,256]{2,0,1:T(1,128)S(1)}, u32[]{:S(2)}, u32[]{:S(2)}) async-start(s32[1,32,256]{2,0,1:T(1,128)} %copy.45), calls=%async_computation | async-start | bytes 65536 | tf_op jit(solution)/shard_map/all_to_all | solution.py:32
  41.7 1.1 copy-start.3
  43.2 5.1 %copy-start.1 = (s32[512,16]{0,1:T(8,128)S(1)}, s32[512,16]{0,1:T(8,128)}, u32[]{:S(2)}) copy-start(s32[512,16]{0,1:T(8,128)} %param.17) | copy-start | bytes 98308
  44.4 21.1 %all-to-all-start.1 = ((bf16[32,256,64]{1,2,0:T(8,128)(2,1)}), bf16[32,256,64]{1,2,0:T(8,128)(2,1)S(1)}, u32[]{:S(2)}, u32[]{:S(2)}) async-start(bf16[32,256,64]{1,2,0:T(8,128)(2,1)} %bitcast.57), calls=%async_computation.1 | async-start | bytes 2097152 | tf_op jit(solution)/shard_map/all_to_all | solution.py:37
  138.3 2.3 %copy-start.4 = (f32[1,64]{1,0:T(1,128)S(1)}, f32[1,64]{1,0:T(1,128)}, u32[]{:S(2)}) copy-start(f32[1,64]{1,0:T(1,128)} %param.14) | copy-start | bytes 772
  140.3 1.6 copy-start.5
  140.3 1.7 %copy-start.2 = (s32[512]{0:T(512)S(1)}, s32[512]{0:T(512)}, u32[]{:S(2)}) copy-start(s32[512]{0:T(512)} %param.18) | copy-start | bytes 6148
where the time goes:
time: 163 us; the launch traced here: 162 us
  matrix products  95.2 us (58%)
  waiting for transfers between devices  24.1 us (15%)
  blocking collectives  15.2 us (9%)
  starting transfers between devices  12.6 us (8%)
  local copies, waits for them, and re-layouts  10 us (6%)
  other arithmetic  4.27 us (3%)
    dot_general x16, matrix products, select_block(): jnp.dot(hot_table, table, preferred_element_type=jnp.float32)  93.7 us
    all_to_all x1, waiting for transfers between devices, local(): lax.all_to_all(owned.reshape(groups, capacity, width), 'node', split_axis...  16.8 us
    all_to_all x1, blocking collectives, local(): lax.all_to_all(hidden, 'head', split_axis=0, concat_axis=1, tiled=True)  15.2 us
    all_to_all x1, starting transfers between devices, local(): lax.all_to_all(request_rows, 'node', split_axis=1, concat_axis=0, tiled=T...  8.58 us
    all_to_all x1, waiting for transfers between devices, local(): lax.all_to_all(request_rows, 'node', split_axis=1, concat_axis=0, tiled=T...  7.25 us
    unnamed x20, local copies, waits for them, and re-layouts  5.08 us
    unnamed x3, other arithmetic  4.06 us
    all_to_all x1, starting transfers between devices, local(): lax.all_to_all(owned.reshape(groups, capacity, width), 'node', split_axis...  3.98 us
  transfers between devices with their start and end apart: 2, of which 2 were waited for; matrix products, arithmetic and copies ran while one was open for 0% of the time, Pallas kernels for 0%

commit v1 on v0

v1 whole, which is shorter than its diff:
```python
import functools

import jax
import jax.numpy as jnp
from jax import lax
from jax.experimental import pallas as pl
from jax.experimental.pallas import tpu as pltpu
from jax.sharding import PartitionSpec as P

MESH = pl.DeviceIdType.MESH
RING = (0, 1, 2, 1)
FEAT, HEADS, DIM, OUT, SLOTS = 100, 8, 64, 512, 16
CAP, HALF, QUART = 256, 128, 64
ROWS = 64
OWNERS = 32


def hops(k):
    return RING[k // 8] + RING[(k // 2) % 4]


PEERS = sorted(range(1, OWNERS), key=lambda k: -hops(k))
FAR = [k for k in PEERS if hops(k) >= 2]
NEAR = [k for k in PEERS if hops(k) < 2]


def shifted(k, sign):
    me = lax.axis_index("node")
    y, x, c = me // 8, (me // 2) % 4, me % 2
    dy, dx, dc = k // 8, (k // 2) % 4, k % 2
    return (((y + sign * dy + 4) % 4) * 4 + (x + sign * dx + 4) % 4) * 2 + (c + sign * dc + 2) % 2


def kernel(
    feat_t, w_t, s_src, s_dst, req, slot_t, cnt, ow, out,
    feat, blk, tab, rx, stage, sendbuf, w_all, sc_all, gath, zf, req_sm, own_sm, slot_sm,
    rq_s, rq_r, rw_s, rw_r, up_s, up_r, dn_s, dn_r, w_s, w_r, sc_s, sc_r, loc,
):
    me, h = lax.axis_index("node"), lax.axis_index("head")
    half = h % 2
    up, down = (h + 1) % HEADS, (h + HEADS - 1) % HEADS

    barrier = pltpu.get_barrier_semaphore()
    for k in PEERS:
        pl.semaphore_signal(barrier, inc=1, device_id=(shifted(k, 1), h), device_id_type=MESH)
    for z in range(1, HEADS):
        pl.semaphore_signal(barrier, inc=1, device_id=(me, (h + z) % HEADS), device_id_type=MESH)

    own_copy = pltpu.make_async_copy(req.at[me], own_sm, loc.at[0])
    own_copy.start()
    slot_copy = pltpu.make_async_copy(slot_t, slot_sm, loc.at[1])
    slot_copy.start()

    blk[...] = jnp.zeros_like(blk)
    for j in range(feat.shape[0] // 128):
        blk[0:FEAT, :] = feat_t[:, j * 128 : (j + 1) * 128].astype(jnp.float32)
        feat[j * 128 : (j + 1) * 128, :] = blk[...].T
    both = jnp.concatenate([s_src[...], s_dst[...]], axis=0)
    sc_all[h] = jnp.concatenate([both, both], axis=1)
    w_all[h] = w_t[...]

    pl.semaphore_wait(barrier, OWNERS - 1 + HEADS - 1)

    sends = []
    for k in PEERS:
        owner = shifted(k, -1)
        if k in FAR:
            src, dst = req.at[owner, pl.ds(half * HALF, HALF)], req_sm.at[k, pl.ds(0, HALF)]
        else:
            src, dst = req.at[owner], req_sm.at[k]
        copy = pltpu.make_async_remote_copy(
            src_ref=src, dst_ref=dst, send_sem=rq_s.at[k], recv_sem=rq_r.at[k],
            device_id=(owner, h), device_id_type=MESH,
        )
        copy.start()
        sends.append(copy)
    along = []
    for z in range(1, HEADS):
        peer = (me, (h + z) % HEADS)
        copy = pltpu.make_async_remote_copy(
            src_ref=w_t, dst_ref=w_all.at[h], send_sem=w_s.at[z], recv_sem=w_r.at[z],
            device_id=peer, device_id_type=MESH,
        )
        copy.start()
        along.append(copy)
        copy = pltpu.make_async_remote_copy(
            src_ref=sc_all.at[h], dst_ref=sc_all.at[h], send_sem=sc_s.at[z], recv_sem=sc_r.at[z],
            device_id=peer, device_id_type=MESH,
        )
        copy.start()
        along.append(copy)

    def pick(table, number, target, base, count):
        def some(b, carry):
            first = b * 16
            for u in range(16):
                i = number(first + u)
                target[pl.ds(base + first + u, 1), :] = table[pl.ds(i, 1), :]
            return carry

        lax.fori_loop(0, count // 16, some, 0)

    own_copy.wait()
    pick(feat, lambda i: own_sm[i], tab, me * CAP, CAP)

    pending = None
    for k in PEERS:
        count = HALF if k in FAR else CAP
        if k in FAR:
            src, dst = req.at[0, pl.ds(0, HALF)], req_sm.at[k, pl.ds(0, HALF)]
        else:
            src, dst = req.at[0], req_sm.at[k]
        pltpu.make_async_remote_copy(
            src_ref=src, dst_ref=dst, send_sem=rq_s.at[k], recv_sem=rq_r.at[k],
            device_id=(shifted(k, 1), h), device_id_type=MESH,
        ).wait_recv()
        pick(feat, lambda i, k=k: req_sm[k, i], stage, 0, count)
        sendbuf[k, 0:count, :] = stage[0:count, :].astype(jnp.bfloat16)
        if pending is not None:
            pending.start()
        if k in FAR:
            dst = rx.at[k, pl.ds(half * HALF, HALF)]
        else:
            dst = rx.at[k]
        pending = pltpu.make_async_remote_copy(
            src_ref=sendbuf.at[k, pl.ds(0, count)], dst_ref=dst, send_sem=rw_s.at[k],
            recv_sem=rw_r.at[k], device_id=(shifted(k, 1), h), device_id_type=MESH,
        )
        sends.append(pending)
    pending.start()

    def spread(k, start, count):
        place = pl.multiple_of(shifted(k, -1) * CAP + start, 64)
        tab[pl.ds(place, count), :] = rx[k, pl.ds(pl.multiple_of(start, 64), count), :].astype(
            jnp.float32
        )

    def hand(k, part, mine, first):
        start = mine * HALF + first * QUART
        ref = rx.at[k, pl.ds(start, QUART)]
        sem = (up_s, up_r) if first == 0 else (dn_s, dn_r)
        return pltpu.make_async_remote_copy(
            src_ref=ref, dst_ref=ref, send_sem=sem[0].at[k], recv_sem=sem[1].at[k],
            device_id=(me, part), device_id_type=MESH,
        )

    for k in FAR:
        pltpu.make_async_remote_copy(
            src_ref=sendbuf.at[k, pl.ds(0, HALF)], dst_ref=rx.at[k, pl.ds(half * HALF, HALF)],
            send_sem=rw_s.at[k], recv_sem=rw_r.at[k], device_id=(me, up), device_id_type=MESH,
        ).wait_recv()
        for part, first in ((up, 0), (down, 1)):
            copy = hand(k, part, half, first)
            copy.start()
            along.append(copy)
        spread(k, half * HALF, HALF)
    for k in NEAR:
        pltpu.make_async_remote_copy(
            src_ref=sendbuf.at[k], dst_ref=rx.at[k], send_sem=rw_s.at[k], recv_sem=rw_r.at[k],
            device_id=(me, up), device_id_type=MESH,
        ).wait_recv()
        spread(k, 0, CAP)
    for k in FAR:
        hand(k, down, 1 - half, 0).wait_recv()
        hand(k, up, 1 - half, 1).wait_recv()
        spread(k, (1 - half) * HALF, HALF)
    for z in range(1, HEADS):
        other = (h + HEADS - z) % HEADS
        pltpu.make_async_remote_copy(
            src_ref=w_t, dst_ref=w_all.at[other], send_sem=w_s.at[z], recv_sem=w_r.at[z],
            device_id=(me, up), device_id_type=MESH,
        ).wait_recv()
        pltpu.make_async_remote_copy(
            src_ref=sc_all.at[h], dst_ref=sc_all.at[other], send_sem=sc_s.at[z],
            recv_sem=sc_r.at[z], device_id=(me, up), device_id_type=MESH,
        ).wait_recv()

    slot_copy.wait()
    for s in range(SLOTS):
        pick(tab, lambda i, s=s: slot_sm[s, h * ROWS + i], gath, s * ROWS, ROWS)

    row = lax.broadcasted_iota(jnp.int32, (2 * HEADS, OUT), 0)
    lane = lax.broadcasted_iota(jnp.int32, (2 * HEADS, OUT), 1)
    score = jnp.zeros((2 * HEADS, OUT), jnp.float32)
    for head in range(HEADS):
        for which in range(2):
            vec = sc_all[head, which : which + 1, :]
            vec = jnp.broadcast_to(jnp.concatenate([vec] * 4, axis=1), (2 * HEADS, OUT))
            hit = (row == which * HEADS + head) & (lane // DIM == head)
            score = jnp.where(hit, vec, score)
    top = score.astype(jnp.bfloat16)
    rest = score - top.astype(jnp.float32)
    mid = rest.astype(jnp.bfloat16)
    low = (rest - mid.astype(jnp.float32)).astype(jnp.bfloat16)

    g = gath[...][:, 0:FEAT].astype(jnp.bfloat16)
    for head in range(HEADS):
        zf[head * DIM : (head + 1) * DIM, :] = lax.dot_general(
            w_all[head], g, (((1,), (1,)), ((), ())), preferred_element_type=jnp.float32
        ).astype(jnp.bfloat16)
    z = zf[...]
    parts = [jnp.dot(piece, z, preferred_element_type=jnp.float32) for piece in (top, mid, low)]
    total = parts[0] + parts[1] + parts[2]
    n = SLOTS * ROWS // 128
    lanes = lax.broadcasted_iota(jnp.int32, (HEADS, 128), 1)
    dst_part = total[HEADS:, 0:128]
    dst_part = jnp.where(lanes < ROWS, dst_part, pltpu.roll(dst_part, ROWS, 1))
    pair = cnt[0:1, pl.ds(pl.multiple_of(h // 2 * 128, 128), 128)]
    pair = jnp.broadcast_to(pair, (HEADS, 128))
    turned = pltpu.roll(pair, ROWS, 1)
    counts = jnp.where((lanes // ROWS) == half, pair, turned)
    logits, lives = [], []
    for j in range(n):
        logit = total[0:HEADS, j * 128 : (j + 1) * 128] + dst_part
        logit = jnp.where(logit > 0, logit, 0.2 * logit)
        live = (2 * j + lanes // ROWS) < counts
        logits.append(jnp.where(live, logit, -1e30))
        lives.append(live)
    peak = functools.reduce(jnp.maximum, logits)
    peak = jnp.maximum(peak, pltpu.roll(peak, ROWS, 1))
    weights = [
        jnp.where(live, jnp.exp(logit - peak), 0.0) for live, logit in zip(lives, logits)
    ]
    norm = functools.reduce(jnp.add, weights)
    norm = norm + pltpu.roll(norm, ROWS, 1)
    alphas = [(w / norm).astype(jnp.bfloat16).astype(jnp.float32) for w in weights]
    hidden = []
    for head in range(HEADS):
        acc = jnp.zeros((DIM, 128), jnp.float32)
        for j in range(n):
            part = zf[head * DIM : (head + 1) * DIM, j * 128 : (j + 1) * 128].astype(jnp.float32)
            acc = acc + part * jnp.broadcast_to(alphas[j][head : head + 1, :], (DIM, 128))
        acc = acc + pltpu.roll(acc, ROWS, 1)
        hidden.append(jnp.where(acc > 0, acc, jnp.exp(jnp.minimum(acc, 0.0)) - 1.0))
    hidden = jnp.concatenate(hidden, axis=0)
    hidden = hidden.T[0:ROWS, :].astype(jnp.bfloat16)
    out[...] = jnp.dot(hidden, ow[...], preferred_element_type=jnp.float32).astype(jnp.bfloat16)

    for copy in sends + along:
        copy.wait_send()


def local(
    features, proj_weight, score_src, score_dst, request_rows, slot_index, slot_count, out_weight
):
    vmem = pl.BlockSpec(memory_space=pltpu.VMEM)
    dma = pltpu.SemaphoreType.DMA
    nodes = features.shape[0]
    return pl.pallas_call(
        kernel,
        out_shape=jax.ShapeDtypeStruct((ROWS, OUT), jnp.bfloat16),
        in_specs=[vmem] * 8,
        out_specs=vmem,
        scratch_shapes=[
            pltpu.VMEM((nodes, 128), jnp.float32),
            pltpu.VMEM((128, 128), jnp.float32),
            pltpu.VMEM((OWNERS * CAP, 128), jnp.float32),
            pltpu.VMEM((OWNERS, CAP, 128), jnp.bfloat16),
            pltpu.VMEM((CAP, 128), jnp.float32),
            pltpu.VMEM((OWNERS, CAP, 128), jnp.bfloat16),
            pltpu.VMEM((HEADS, DIM, FEAT), jnp.bfloat16),
            pltpu.VMEM((HEADS, 2, 128), jnp.float32),
            pltpu.VMEM((SLOTS * ROWS, 128), jnp.float32),
            pltpu.VMEM((OUT, SLOTS * ROWS), jnp.bfloat16),
            pltpu.SMEM((OWNERS, CAP), jnp.int32),
            pltpu.SMEM((CAP,), jnp.int32),
            pltpu.SMEM((SLOTS, 512), jnp.int32),
        ]
        + [dma((OWNERS,))] * 8
        + [dma((HEADS,))] * 4
        + [dma((2,))],
        compiler_params=pltpu.CompilerParams(
            collective_id=0, has_side_effects=True, vmem_limit_bytes=48 * 1024 * 1024
        ),
        name="layer",
    )(
        features.T, proj_weight.T, score_src, score_dst, request_rows.reshape(OWNERS, CAP),
        slot_index.T, slot_count.reshape(1, -1), out_weight,
    )


def solution(mesh):
    in_specs = (
        P("node", None),
        P(None, "head"),
        P("head", None),
        P("head", None),
        P("node", None, None),
        P("node", None),
        P("node"),
        P(),
    )
    out_specs = P(("node", "head"), None)
    return jax.shard_map(local, mesh=mesh, in_specs=in_specs, out_specs=out_specs, check_vma=False)
```

time: 163 us -> 50.8 us (0.31)
  matrix products: 95.2 us -> 0 us
  Pallas kernels: 0 us -> 44.7 us
  waiting for transfers between devices: 24.1 us -> 0 us
  blocking collectives: 15.2 us -> 0 us
  starting transfers between devices: 12.6 us -> 0 us
  local copies, waits for them, and re-layouts: 10 us -> 5.59 us
  other arithmetic: 4.27 us -> 0 us
    dot_general x19 -> x0, matrix products: 95.2 us -> none  [the longest x16 93.7 us: select_block(): jnp.dot(hot_table, table, preferred_element_type=jnp.float32)]
    pallas_call x0 -> x1, Pallas kernels: none -> 44.7 us  [local(): pl.pallas_call(kernel, out_shape=jax.ShapeDtypeStruct((ROWS, OUT), jnp.bf...]
    all_to_all x2 -> x0, waiting for transfers between devices: 24.1 us -> none  [the longest x1 16.8 us: local(): lax.all_to_all(owned.reshape(groups, capacity, width), 'node', split_axis...]
    all_to_all x1 -> x0, blocking collectives: 15.2 us -> none  [local(): lax.all_to_all(hidden, 'head', split_axis=0, concat_axis=1, tiled=True)]
    all_to_all x2 -> x0, starting transfers between devices: 12.6 us -> none  [the longest x1 8.58 us: local(): lax.all_to_all(request_rows, 'node', split_axis=1, concat_axis=0, tiled=T...]
    unnamed x3 -> x0, other arithmetic: 4.06 us -> none
    while x2 -> x0, local copies, waits for them, and re-layouts: 2.94 us -> none  [pick_rows(): lax.map(select_block, row_index.reshape(total // block_rows, block_rows))]
    unnamed x20 -> x17, local copies, waits for them, and re-layouts: 5.08 us -> 5.59 us
  transfers between devices with their start and end apart: 2 -> 0, of which waited for: 2 -> 0; matrix products, arithmetic and copies ran while one was open for 0% -> 0% of each run, Pallas kernels for 0% -> 0%
where the time goes in v1:
time: 50.8 us; the launch traced here: 50.3 us
  Pallas kernels  44.7 us (88%)
  local copies, waits for them, and re-layouts  5.59 us (11%)
    pallas_call x1, Pallas kernels, local(): pl.pallas_call(kernel, out_shape=jax.ShapeDtypeStruct((ROWS, OUT), jnp.bf...  44.7 us
    unnamed x17, local copies, waits for them, and re-layouts  5.59 us

profile of v1, /device:TPU:1, one launch (start us, length us, event | category | flops | bytes accessed | tf_op | source)
XLA Modules:
  0.0 50.3 jit_solution(2675286399579988416)
XLA Ops:
  0.0 0.0 copy-start.5
  0.0 0.0 copy-start.6
  0.0 0.0 copy-start.7
  0.0 0.7 %copy-done.5 = s32[512]{0:T(512)S(1)} copy-done((s32[512]{0:T(512)S(1)}, s32[512]{0:T(512)}, u32[]{:S(2)}) %copy-start.5) | copy-done | bytes 2072
  0.7 0.0 copy-done.6
  0.7 0.0 copy-done.7
  0.7 0.0 copy-start
  0.7 1.0 %copy-done = bf16[512,512]{1,0:T(8,128)(2,1)S(1)} copy-done((bf16[512,512]{1,0:T(8,128)(2,1)S(1)}, bf16[512,512]{1,0:T(8,128)(2,1)}, u32[]{:S(2)}) %copy-start) | copy-done | bytes 524312
  1.7 0.0 copy-start.1
  1.7 1.0 %copy-done.1 = bf16[2048,100]{0,1:T(8,128)(2,1)S(1)} copy-done((bf16[2048,100]{0,1:T(8,128)(2,1)S(1)}, bf16[2048,100]{0,1:T(8,128)(2,1)}, u32[]{:S(2)}) %copy-start.1) | copy-done | bytes 409624
  2.7 0.0 copy-start.2
  2.7 0.8 %copy-done.2 = s32[1,32,256]{2,1,0:T(8,128)S(1)} copy-done((s32[1,32,256]{2,1,0:T(8,128)S(1)}, s32[1,32,256]{2,1,0:T(8,128)}, u32[]{:S(2)}) %copy-start.2) | copy-done | bytes 32792
  3.5 0.0 copy-start.3
  3.5 0.8 %copy-done.3 = s32[512,16]{0,1:T(8,128)S(1)} copy-done((s32[512,16]{0,1:T(8,128)S(1)}, s32[512,16]{0,1:T(8,128)}, u32[]{:S(2)}) %copy-start.3) | copy-done | bytes 32792
  4.3 0.0 copy-start.4
  4.3 0.7 %copy-done.4 = bf16[100,64]{0,1:T(8,128)(2,1)S(1)} copy-done((bf16[100,64]{0,1:T(8,128)(2,1)S(1)}, bf16[100,64]{0,1:T(8,128)(2,1)}, u32[]{:S(2)}) %copy-start.4) | copy-done | bytes 12824
  5.0 44.7 %layer.1 = bf16[64,512]{1,0:T(8,128)(2,1)S(1)} custom-call(bf16[100,2048]{1,0:T(8,128)(2,1)S(1)} %bitcast.5, bf16[64,100]{1,0:T(8,128)(2,1)S(1)} %bitcast.8, f32[1,64]{1,0:T(1,128)S(1)} %copy-done.6, f32[1,64]{1,0:T(1,128)S(1)} %copy-done.7, s32[32,256]{1,0:T(8,128)S(1)} %bitcast.6, s32[16,512]{1,0:T(8,128)S(1)} %bitcast.7, s32[1,512]{1,0:T(1,128)S(1)} %bitcast.9, ...), custom_call_target="tpu_custom_call" | custom-call | tf_op jit(solution)/shard_map/layer/pallas_call | solution.py:249
  49.6 0.6 %copy.10 = bf16[64,512]{1,0:T(8,128)(2,1)} copy(bf16[64,512]{1,0:T(8,128)(2,1)S(1)} %layer.1) | data formatting | bytes 131072
Async XLA Ops:
  0.0 0.7 %copy-start.5 = (s32[512]{0:T(512)S(1)}, s32[512]{0:T(512)}, u32[]{:S(2)}) copy-start(s32[512]{0:T(512)} %param.14) | copy-start | bytes 6148
  0.0 0.7 %copy-start.6 = (f32[1,64]{1,0:T(1,128)S(1)}, f32[1,64]{1,0:T(1,128)}, u32[]{:S(2)}) copy-start(f32[1,64]{1,0:T(1,128)} %s_src.1) | copy-start | bytes 772
  0.0 0.7 %copy-start.7 = (f32[1,64]{1,0:T(1,128)S(1)}, f32[1,64]{1,0:T(1,128)}, u32[]{:S(2)}) copy-start(f32[1,64]{1,0:T(1,128)} %s_dst.1) | copy-start | bytes 772
  0.7 1.0 %copy-start = (bf16[512,512]{1,0:T(8,128)(2,1)S(1)}, bf16[512,512]{1,0:T(8,128)(2,1)}, u32[]{:S(2)}) copy-start(bf16[512,512]{1,0:T(8,128)(2,1)} %ow.1) | copy-start | bytes 1572868
  1.7 1.0 %copy-start.1 = (bf16[2048,100]{0,1:T(8,128)(2,1)S(1)}, bf16[2048,100]{0,1:T(8,128)(2,1)}, u32[]{:S(2)}) copy-start(bf16[2048,100]{0,1:T(8,128)(2,1)} %param.8) | copy-start | bytes 1228804
  2.7 0.8 %copy-start.2 = (s32[1,32,256]{2,1,0:T(8,128)S(1)}, s32[1,32,256]{2,1,0:T(8,128)}, u32[]{:S(2)}) copy-start(s32[1,32,256]{2,1,0:T(8,128)} %param.12) | copy-start | bytes 98308
  3.5 0.8 %copy-start.3 = (s32[512,16]{0,1:T(8,128)S(1)}, s32[512,16]{0,1:T(8,128)}, u32[]{:S(2)}) copy-start(s32[512,16]{0,1:T(8,128)} %param.13) | copy-start | bytes 98308
  4.3 0.7 %copy-start.4 = (bf16[100,64]{0,1:T(8,128)(2,1)S(1)}, bf16[100,64]{0,1:T(8,128)(2,1)}, u32[]{:S(2)}) copy-start(bf16[100,64]{0,1:T(8,128)(2,1)} %param.9) | copy-start | bytes 38404

commit v2 on v1

--- a/solution.py
+++ b/solution.py
@@ -33,6 +33,7 @@
 
 def kernel(
     feat_t, w_t, s_src, s_dst, req, slot_t, cnt, ow, out,
+    feat_in, req_in, sc_in, cnt_in, ow_in,
     feat, blk, tab, rx, stage, sendbuf, w_all, sc_all, gath, zf, req_sm, own_sm, slot_sm,
     rq_s, rq_r, rw_s, rw_r, up_s, up_r, dn_s, dn_r, w_s, w_r, sc_s, sc_r, loc,
 ):
@@ -46,39 +47,63 @@
     for z in range(1, HEADS):
         pl.semaphore_signal(barrier, inc=1, device_id=(me, (h + z) % HEADS), device_id_type=MESH)
 
-    own_copy = pltpu.make_async_copy(req.at[me], own_sm, loc.at[0])
-    own_copy.start()
-    slot_copy = pltpu.make_async_copy(slot_t, slot_sm, loc.at[1])
-    slot_copy.start()
+    lane_block = pl.multiple_of(h // 2 * 128, 128)
+    loads = [
+        pltpu.make_async_copy(src, dst, loc.at[n])
+        for n, (src, dst) in enumerate(
+            (
+                (feat_t, feat_in),
+                (req, req_in),
+                (req.at[me, pl.ds(0, HALF)], own_sm.at[0]),
+                (req.at[me, pl.ds(HALF, HALF)], own_sm.at[1]),
+                (w_t, w_all.at[h]),
+                (s_src, sc_in.at[0]),
+                (s_dst, sc_in.at[1]),
+                (slot_t.at[:, pl.ds(lane_block, 128)], slot_sm),
+                (cnt.at[:, pl.ds(lane_block, 128)], cnt_in),
+                (ow, ow_in),
+            )
+        )
+    ]
+    for load in loads:
+        load.start()
+    feat_load, req_load, own_load, own_load2, w_load, src_load, dst_load, slot_load, cnt_load, ow_load = loads
 
     blk[...] = jnp.zeros_like(blk)
+    feat_load.wait()
     for j in range(feat.shape[0] // 128):
-        blk[0:FEAT, :] = feat_t[:, j * 128 : (j + 1) * 128].astype(jnp.float32)
+        blk[0:FEAT, :] = feat_in[:, j * 128 : (j + 1) * 128].astype(jnp.float32)
         feat[j * 128 : (j + 1) * 128, :] = blk[...].T
-    both = jnp.concatenate([s_src[...], s_dst[...]], axis=0)
+    src_load.wait()
+    dst_load.wait()
+    both = jnp.concatenate([sc_in[0], sc_in[1]], axis=0)
     sc_all[h] = jnp.concatenate([both, both], axis=1)
-    w_all[h] = w_t[...]
+    w_load.wait()
+    req_load.wait()
 
     pl.semaphore_wait(barrier, OWNERS - 1 + HEADS - 1)
+
+    def ask(k, part, owner, target):
+        column = half if k in FAR else part
+        return pltpu.make_async_remote_copy(
+            src_ref=req_in.at[owner, pl.ds(pl.multiple_of(column * HALF, HALF), HALF)],
+            dst_ref=req_sm.at[k, part],
+            send_sem=rq_s.at[k, part], recv_sem=rq_r.at[k, part],
+            device_id=(target, h), device_id_type=MESH,
+        )
 
     sends = []
     for k in PEERS:
         owner = shifted(k, -1)
-        if k in FAR:
-            src, dst = req.at[owner, pl.ds(half * HALF, HALF)], req_sm.at[k, pl.ds(0, HALF)]
-        else:
-            src, dst = req.at[owner], req_sm.at[k]
-        copy = pltpu.make_async_remote_copy(
-            src_ref=src, dst_ref=dst, send_sem=rq_s.at[k], recv_sem=rq_r.at[k],
-            device_id=(owner, h), device_id_type=MESH,
-        )
-        copy.start()
-        sends.append(copy)
+        for part in range(1 if k in FAR else 2):
+            copy = ask(k, part, owner, owner)
+            copy.start()
+            sends.append(copy)
     along = []
     for z in range(1, HEADS):
         peer = (me, (h + z) % HEADS)
         copy = pltpu.make_async_remote_copy(
-            src_ref=w_t, dst_ref=w_all.at[h], send_sem=w_s.at[z], recv_sem=w_r.at[z],
+            src_ref=w_all.at[h], dst_ref=w_all.at[h], send_sem=w_s.at[z], recv_sem=w_r.at[z],
             device_id=peer, device_id_type=MESH,
         )
         copy.start()
@@ -91,30 +116,29 @@
         along.append(copy)
 
     def pick(table, number, target, base, count):
-        def some(b, carry):
-            first = b * 16
-            for u in range(16):
-                i = number(first + u)
-                target[pl.ds(base + first + u, 1), :] = table[pl.ds(i, 1), :]
-            return carry
-
-        lax.fori_loop(0, count // 16, some, 0)
-
-    own_copy.wait()
-    pick(feat, lambda i: own_sm[i], tab, me * CAP, CAP)
+        for u in range(count):
+            target[pl.ds(base + u, 1), :] = table[pl.ds(number(u), 1), :]
+
+    own_load.wait()
+    own_load2.wait()
+
+    def own(part, carry):
+        pick(feat, lambda u: own_sm[part, u], tab, me * CAP + part * HALF, HALF)
+        return carry
+
+    lax.fori_loop(0, 2, own, 0)
 
     pending = None
     for k in PEERS:
         count = HALF if k in FAR else CAP
-        if k in FAR:
-            src, dst = req.at[0, pl.ds(0, HALF)], req_sm.at[k, pl.ds(0, HALF)]
-        else:
-            src, dst = req.at[0], req_sm.at[k]
-        pltpu.make_async_remote_copy(
-            src_ref=src, dst_ref=dst, send_sem=rq_s.at[k], recv_sem=rq_r.at[k],
-            device_id=(shifted(k, 1), h), device_id_type=MESH,
-        ).wait_recv()
-        pick(feat, lambda i, k=k: req_sm[k, i], stage, 0, count)
+        for part in range(count // HALF):
+            ask(k, part, 0, shifted(k, 1)).wait_recv()
+
+        def some(part, carry, k=k):
+            pick(feat, lambda u: req_sm[k, part, u], stage, part * HALF, HALF)
+            return carry
+
+        lax.fori_loop(0, count // HALF, some, 0)
         sendbuf[k, 0:count, :] = stage[0:count, :].astype(jnp.bfloat16)
         if pending is not None:
             pending.start()
@@ -167,7 +191,7 @@
     for z in range(1, HEADS):
         other = (h + HEADS - z) % HEADS
         pltpu.make_async_remote_copy(
-            src_ref=w_t, dst_ref=w_all.at[other], send_sem=w_s.at[z], recv_sem=w_r.at[z],
+            src_ref=w_all.at[h], dst_ref=w_all.at[other], send_sem=w_s.at[z], recv_sem=w_r.at[z],
             device_id=(me, up), device_id_type=MESH,
         ).wait_recv()
         pltpu.make_async_remote_copy(
@@ -175,9 +199,16 @@
             recv_sem=sc_r.at[z], device_id=(me, up), device_id_type=MESH,
         ).wait_recv()
 
-    slot_copy.wait()
-    for s in range(SLOTS):
-        pick(tab, lambda i, s=s: slot_sm[s, h * ROWS + i], gath, s * ROWS, ROWS)
+    slot_load.wait()
+    for side in range(2):
+
+        @pl.when(half == side)
+        def _(side=side):
+            def some(s, carry):
+                pick(tab, lambda u: slot_sm[s, side * ROWS + u], gath, s * ROWS, ROWS)
+                return carry
+
+            lax.fori_loop(0, SLOTS, some, 0)
 
     row = lax.broadcasted_iota(jnp.int32, (2 * HEADS, OUT), 0)
     lane = lax.broadcasted_iota(jnp.int32, (2 * HEADS, OUT), 1)
@@ -205,8 +236,8 @@
     lanes = lax.broadcasted_iota(jnp.int32, (HEADS, 128), 1)
     dst_part = total[HEADS:, 0:128]
     dst_part = jnp.where(lanes < ROWS, dst_part, pltpu.roll(dst_part, ROWS, 1))
-    pair = cnt[0:1, pl.ds(pl.multiple_of(h // 2 * 128, 128), 128)]
-    pair = jnp.broadcast_to(pair, (HEADS, 128))
+    cnt_load.wait()
+    pair = jnp.broadcast_to(cnt_in[...], (HEADS, 128))
     turned = pltpu.roll(pair, ROWS, 1)
     counts = jnp.where((lanes // ROWS) == half, pair, turned)
     logits, lives = [], []
@@ -234,7 +265,8 @@
         hidden.append(jnp.where(acc > 0, acc, jnp.exp(jnp.minimum(acc, 0.0)) - 1.0))
     hidden = jnp.concatenate(hidden, axis=0)
     hidden = hidden.T[0:ROWS, :].astype(jnp.bfloat16)
-    out[...] = jnp.dot(hidden, ow[...], preferred_element_type=jnp.float32).astype(jnp.bfloat16)
+    ow_load.wait()
+    out[...] = jnp.dot(hidden, ow_in[...], preferred_element_type=jnp.float32).astype(jnp.bfloat16)
 
     for copy in sends + along:
         copy.wait_send()
@@ -249,9 +281,14 @@
     return pl.pallas_call(
         kernel,
         out_shape=jax.ShapeDtypeStruct((ROWS, OUT), jnp.bfloat16),
-        in_specs=[vmem] * 8,
+        in_specs=[pl.BlockSpec(memory_space=pltpu.HBM)] * 8,
         out_specs=vmem,
         scratch_shapes=[
+            pltpu.VMEM((FEAT, nodes), jnp.bfloat16),
+            pltpu.VMEM((OWNERS, CAP), jnp.int32),
+            pltpu.VMEM((2, 1, DIM), jnp.float32),
+            pltpu.VMEM((1, 128), jnp.int32),
+            pltpu.VMEM((OUT, OUT), jnp.bfloat16),
             pltpu.VMEM((nodes, 128), jnp.float32),
             pltpu.VMEM((128, 128), jnp.float32),
             pltpu.VMEM((OWNERS * CAP, 128), jnp.float32),
@@ -262,15 +299,16 @@
             pltpu.VMEM((HEADS, 2, 128), jnp.float32),
             pltpu.VMEM((SLOTS * ROWS, 128), jnp.float32),
             pltpu.VMEM((OUT, SLOTS * ROWS), jnp.bfloat16),
-            pltpu.SMEM((OWNERS, CAP), jnp.int32),
-            pltpu.SMEM((CAP,), jnp.int32),
-            pltpu.SMEM((SLOTS, 512), jnp.int32),
+            pltpu.SMEM((OWNERS, 2, HALF), jnp.int32),
+            pltpu.SMEM((2, HALF), jnp.int32),
+            pltpu.SMEM((SLOTS, 128), jnp.int32),
         ]
-        + [dma((OWNERS,))] * 8
+        + [dma((OWNERS, 2))] * 2
+        + [dma((OWNERS,))] * 6
         + [dma((HEADS,))] * 4
-        + [dma((2,))],
+        + [dma((10,))],
         compiler_params=pltpu.CompilerParams(
-            collective_id=0, has_side_effects=True, vmem_limit_bytes=48 * 1024 * 1024
+            collective_id=0, has_side_effects=True, vmem_limit_bytes=60 * 1024 * 1024
         ),
         name="layer",
     )(

time: 50.8 us -> 42.4 us (0.83)
  local copies, waits for them, and re-layouts: 5.59 us -> 1.47 us
  Pallas kernels: 44.7 us -> 40.8 us
    unnamed x17 -> x1, local copies, waits for them, and re-layouts: 5.59 us -> 1.47 us
    pallas_call x1, Pallas kernels: 44.7 us -> 40.8 us  [local(): pl.pallas_call(kernel, out_shape=jax.ShapeDtypeStruct((ROWS, OUT), jnp.bf...]
where the time goes in v2:
time: 42.4 us; the launch traced here: 42.3 us
  Pallas kernels  40.8 us (96%)
  local copies, waits for them, and re-layouts  1.47 us (3%)
    pallas_call x1, Pallas kernels, local(): pl.pallas_call(kernel, out_shape=jax.ShapeDtypeStruct((ROWS, OUT), jnp.bf...  40.8 us
    unnamed x1, local copies, waits for them, and re-layouts  1.47 us

profile of v2, /device:TPU:1, one launch (start us, length us, event | category | flops | bytes accessed | tf_op | source)
XLA Modules:
  0.0 42.3 jit_solution(9782966029208545902)
XLA Ops:
  0.0 40.8 %layer.1 = bf16[64,512]{1,0:T(8,128)(2,1)} custom-call(bf16[100,2048]{1,0:T(8,128)(2,1)} %bitcast.5, bf16[64,100]{1,0:T(8,128)(2,1)} %bitcast.8, f32[1,64]{1,0:T(1,128)} %s_src.1, f32[1,64]{1,0:T(1,128)} %s_dst.1, s32[32,256]{1,0:T(8,128)} %bitcast.6, s32[16,512]{1,0:T(8,128)} %bitcast.7, s32[1,512]{1,0:T(1,128)} %bitcast.9, bf16[512,512]{1,0:T(8,128)(2,1)} %ow.1), custom_call_target="tpu_custom_call" | custom-call | tf_op jit(solution)/shard_map/layer/pallas_call | solution.py:281
  40.8 1.5 %copy.10 = bf16[64,512]{1,0:T(8,128)(2,1)} copy(bf16[64,512]{1,0:T(8,128)(2,1)} %layer.1) | data formatting | bytes 131072

commit v3 on v2

--- a/solution.py
+++ b/solution.py
@@ -10,7 +10,8 @@
 MESH = pl.DeviceIdType.MESH
 RING = (0, 1, 2, 1)
 FEAT, HEADS, DIM, OUT, SLOTS = 100, 8, 64, 512, 16
-CAP, HALF, QUART = 256, 128, 64
+CAP, HALF = 256, 128
+PACK = 104
 ROWS = 64
 OWNERS = 32
 
@@ -19,9 +20,10 @@
     return RING[k // 8] + RING[(k // 2) % 4]
 
 
-PEERS = sorted(range(1, OWNERS), key=lambda k: -hops(k))
-FAR = [k for k in PEERS if hops(k) >= 2]
-NEAR = [k for k in PEERS if hops(k) < 2]
+FAR = sorted((k for k in range(1, OWNERS) if hops(k) >= 2), key=lambda k: -hops(k))
+NEAR = [2, 6, 8, 24, 3, 7, 9, 25, 1]
+PEERS = FAR + NEAR
+HELD = 6
 
 
 def shifted(k, sign):
@@ -31,10 +33,42 @@
     return (((y + sign * dy + 4) % 4) * 4 + (x + sign * dx + 4) % 4) * 2 + (c + sign * dc + 2) % 2
 
 
+def pack(x):
+    lane = lax.broadcasted_iota(jnp.int32, (8, 128), 1)
+    group = [x[8 * i : 8 * i + 8] for i in range(16)]
+    rows = [jnp.where(lane < 64, group[i], pltpu.roll(group[8 + i], 64, 1)) for i in range(8)]
+    for i in range(4):
+        acc = group[8 + i]
+        for q in (0, 1, 3):
+            moved = pltpu.roll(group[4 * q + i], (32 * q - 64) % 128, 1)
+            acc = jnp.where(lane // 32 == q, moved, acc)
+        rows.append(acc)
+    acc = group[12]
+    for q in range(16):
+        if q != 12:
+            acc = jnp.where(lane // 8 == q, pltpu.roll(group[q], (8 * q - 96) % 128, 1), acc)
+    rows.append(acc)
+    return jnp.concatenate(rows, axis=0)
+
+
+def unpack(y):
+    lane = lax.broadcasted_iota(jnp.int32, (8, 128), 1)
+    group = [y[8 * i : 8 * i + 8] for i in range(13)]
+    rows = []
+    for i in range(16):
+        first = group[i] if i < 8 else pltpu.roll(group[i - 8], 64, 1)
+        second = group[8 + i % 4]
+        if i // 4 != 2:
+            second = pltpu.roll(second, (64 - 32 * (i // 4)) % 128, 1)
+        third = group[12] if i == 12 else pltpu.roll(group[12], (96 - 8 * i) % 128, 1)
+        rows.append(jnp.where(lane < 64, first, jnp.where(lane < 96, second, third)))
+    return jnp.concatenate(rows, axis=0)
+
+
 def kernel(
     feat_t, w_t, s_src, s_dst, req, slot_t, cnt, ow, out,
     feat_in, req_in, sc_in, cnt_in, ow_in,
-    feat, blk, tab, rx, stage, sendbuf, w_all, sc_all, gath, zf, req_sm, own_sm, slot_sm,
+    feat, blk, tab, rx, stage, sendbuf, w_all, sc_all, gath, zf, sc_mat, req_sm, own_sm, slot_sm,
     rq_s, rq_r, rw_s, rw_r, up_s, up_r, dn_s, dn_r, w_s, w_r, sc_s, sc_r, loc,
 ):
     me, h = lax.axis_index("node"), lax.axis_index("head")
@@ -128,66 +162,54 @@
 
     lax.fori_loop(0, 2, own, 0)
 
-    pending = None
-    for k in PEERS:
+    def give(k):
+        src, dst = (sendbuf.at[k, 0], rx.at[k, half]) if k in FAR else (sendbuf.at[k], rx.at[k])
+        return pltpu.make_async_remote_copy(
+            src_ref=src, dst_ref=dst, send_sem=rw_s.at[k],
+            recv_sem=rw_r.at[k], device_id=(shifted(k, 1), h), device_id_type=MESH,
+        )
+
+    def send(k):
+        copy = give(k)
+        copy.start()
+        sends.append(copy)
+
+    for n, k in enumerate(PEERS):
         count = HALF if k in FAR else CAP
         for part in range(count // HALF):
             ask(k, part, 0, shifted(k, 1)).wait_recv()
 
         def some(part, carry, k=k):
-            pick(feat, lambda u: req_sm[k, part, u], stage, part * HALF, HALF)
+            pick(feat, lambda u: req_sm[k, part, u], stage, 0, HALF)
+            sendbuf[k, part] = pack(stage[...]).astype(jnp.bfloat16)
             return carry
 
         lax.fori_loop(0, count // HALF, some, 0)
-        sendbuf[k, 0:count, :] = stage[0:count, :].astype(jnp.bfloat16)
-        if pending is not None:
-            pending.start()
-        if k in FAR:
-            dst = rx.at[k, pl.ds(half * HALF, HALF)]
-        else:
-            dst = rx.at[k]
-        pending = pltpu.make_async_remote_copy(
-            src_ref=sendbuf.at[k, pl.ds(0, count)], dst_ref=dst, send_sem=rw_s.at[k],
-            recv_sem=rw_r.at[k], device_id=(shifted(k, 1), h), device_id_type=MESH,
-        )
-        sends.append(pending)
-    pending.start()
-
-    def spread(k, start, count):
-        place = pl.multiple_of(shifted(k, -1) * CAP + start, 64)
-        tab[pl.ds(place, count), :] = rx[k, pl.ds(pl.multiple_of(start, 64), count), :].astype(
-            jnp.float32
-        )
+        if 1 <= n <= len(FAR):
+            send(PEERS[n - 1])
+
+    def spread(k, part):
+        place = pl.multiple_of(shifted(k, -1) * CAP + part * HALF, HALF)
+        tab[pl.ds(place, HALF), :] = unpack(rx[k, part].astype(jnp.float32))
 
     def hand(k, part, mine, first):
-        start = mine * HALF + first * QUART
-        ref = rx.at[k, pl.ds(start, QUART)]
+        start, count = (0, 48) if first == FAR.index(k) % 2 else (48, PACK - 48)
+        ref = rx.at[k, mine, pl.ds(start, count)]
         sem = (up_s, up_r) if first == 0 else (dn_s, dn_r)
         return pltpu.make_async_remote_copy(
             src_ref=ref, dst_ref=ref, send_sem=sem[0].at[k], recv_sem=sem[1].at[k],
             device_id=(me, part), device_id_type=MESH,
         )
 
-    for k in FAR:
-        pltpu.make_async_remote_copy(
-            src_ref=sendbuf.at[k, pl.ds(0, HALF)], dst_ref=rx.at[k, pl.ds(half * HALF, HALF)],
-            send_sem=rw_s.at[k], recv_sem=rw_r.at[k], device_id=(me, up), device_id_type=MESH,
-        ).wait_recv()
+    for n, k in enumerate(FAR):
+        give(k).wait_recv()
         for part, first in ((up, 0), (down, 1)):
             copy = hand(k, part, half, first)
             copy.start()
             along.append(copy)
-        spread(k, half * HALF, HALF)
-    for k in NEAR:
-        pltpu.make_async_remote_copy(
-            src_ref=sendbuf.at[k], dst_ref=rx.at[k], send_sem=rw_s.at[k], recv_sem=rw_r.at[k],
-            device_id=(me, up), device_id_type=MESH,
-        ).wait_recv()
-        spread(k, 0, CAP)
-    for k in FAR:
-        hand(k, down, 1 - half, 0).wait_recv()
-        hand(k, up, 1 - half, 1).wait_recv()
-        spread(k, (1 - half) * HALF, HALF)
+        spread(k, half)
+        if HELD <= n < HELD + len(NEAR):
+            send(NEAR[n - HELD])
     for z in range(1, HEADS):
         other = (h + HEADS - z) % HEADS
         pltpu.make_async_remote_copy(
@@ -198,17 +220,6 @@
             src_ref=sc_all.at[h], dst_ref=sc_all.at[other], send_sem=sc_s.at[z],
             recv_sem=sc_r.at[z], device_id=(me, up), device_id_type=MESH,
         ).wait_recv()
-
-    slot_load.wait()
-    for side in range(2):
-
-        @pl.when(half == side)
-        def _(side=side):
-            def some(s, carry):
-                pick(tab, lambda u: slot_sm[s, side * ROWS + u], gath, s * ROWS, ROWS)
-                return carry
-
-            lax.fori_loop(0, SLOTS, some, 0)
 
     row = lax.broadcasted_iota(jnp.int32, (2 * HEADS, OUT), 0)
     lane = lax.broadcasted_iota(jnp.int32, (2 * HEADS, OUT), 1)
@@ -223,15 +234,39 @@
     rest = score - top.astype(jnp.float32)
     mid = rest.astype(jnp.bfloat16)
     low = (rest - mid.astype(jnp.float32)).astype(jnp.bfloat16)
+    for n, piece in enumerate((top, mid, low)):
+        sc_mat[n * 2 * HEADS : (n + 1) * 2 * HEADS, :] = piece
+
+    for k in NEAR:
+        give(k).wait_recv()
+
+        def both_halves(part, carry, k=k):
+            spread(k, part)
+            return carry
+
+        lax.fori_loop(0, 2, both_halves, 0)
+    for k in FAR:
+        hand(k, down, 1 - half, 0).wait_recv()
+        hand(k, up, 1 - half, 1).wait_recv()
+        spread(k, 1 - half)
+    slot_load.wait()
+    for side in range(2):
+
+        @pl.when(half == side)
+        def _(side=side):
+            def some(s, carry):
+                pick(tab, lambda u: slot_sm[s, side * ROWS + u], gath, s * ROWS, ROWS)
+                return carry
+
+            lax.fori_loop(0, SLOTS, some, 0)
 
     g = gath[...][:, 0:FEAT].astype(jnp.bfloat16)
-    for head in range(HEADS):
-        zf[head * DIM : (head + 1) * DIM, :] = lax.dot_general(
-            w_all[head], g, (((1,), (1,)), ((), ())), preferred_element_type=jnp.float32
-        ).astype(jnp.bfloat16)
-    z = zf[...]
-    parts = [jnp.dot(piece, z, preferred_element_type=jnp.float32) for piece in (top, mid, low)]
-    total = parts[0] + parts[1] + parts[2]
+    zf[...] = lax.dot_general(
+        w_all[...].reshape(OUT, FEAT), g, (((1,), (1,)), ((), ())),
+        preferred_element_type=jnp.float32,
+    ).astype(jnp.bfloat16)
+    parts = jnp.dot(sc_mat[...], zf[...], preferred_element_type=jnp.float32)
+    total = parts[0:16] + parts[16:32] + parts[32:48]
     n = SLOTS * ROWS // 128
     lanes = lax.broadcasted_iota(jnp.int32, (HEADS, 128), 1)
     dst_part = total[HEADS:, 0:128]
@@ -292,13 +327,14 @@
             pltpu.VMEM((nodes, 128), jnp.float32),
             pltpu.VMEM((128, 128), jnp.float32),
             pltpu.VMEM((OWNERS * CAP, 128), jnp.float32),
-            pltpu.VMEM((OWNERS, CAP, 128), jnp.bfloat16),
-            pltpu.VMEM((CAP, 128), jnp.float32),
-            pltpu.VMEM((OWNERS, CAP, 128), jnp.bfloat16),
+            pltpu.VMEM((OWNERS, 2, PACK, 128), jnp.bfloat16),
+            pltpu.VMEM((HALF, 128), jnp.float32),
+            pltpu.VMEM((OWNERS, 2, PACK, 128), jnp.bfloat16),
             pltpu.VMEM((HEADS, DIM, FEAT), jnp.bfloat16),
             pltpu.VMEM((HEADS, 2, 128), jnp.float32),
             pltpu.VMEM((SLOTS * ROWS, 128), jnp.float32),
             pltpu.VMEM((OUT, SLOTS * ROWS), jnp.bfloat16),
+            pltpu.VMEM((6 * HEADS, OUT), jnp.bfloat16),
             pltpu.SMEM((OWNERS, 2, HALF), jnp.int32),
             pltpu.SMEM((2, HALF), jnp.int32),
             pltpu.SMEM((SLOTS, 128), jnp.int32),

time: 42.4 us -> 40.8 us (0.962)
  Pallas kernels: 40.8 us -> 39.2 us
    pallas_call x1, Pallas kernels: 40.8 us -> 39.2 us  [local(): pl.pallas_call(kernel, out_shape=jax.ShapeDtypeStruct((ROWS, OUT), jnp.bf...]
where the time goes in v3:
time: 40.8 us; the launch traced here: 40.7 us
  Pallas kernels  39.2 us (96%)
  local copies, waits for them, and re-layouts  1.47 us (4%)
    pallas_call x1, Pallas kernels, local(): pl.pallas_call(kernel, out_shape=jax.ShapeDtypeStruct((ROWS, OUT), jnp.bf...  39.2 us
    unnamed x1, local copies, waits for them, and re-layouts  1.47 us

profile of v3, /device:TPU:1, one launch (start us, length us, event | category | flops | bytes accessed | tf_op | source)
XLA Modules:
  0.0 40.7 jit_solution(422918596828089856)
XLA Ops:
  0.0 39.2 %layer.1 = bf16[64,512]{1,0:T(8,128)(2,1)} custom-call(bf16[100,2048]{1,0:T(8,128)(2,1)} %bitcast.5, bf16[64,100]{1,0:T(8,128)(2,1)} %bitcast.8, f32[1,64]{1,0:T(1,128)} %s_src.1, f32[1,64]{1,0:T(1,128)} %s_dst.1, s32[32,256]{1,0:T(8,128)} %bitcast.6, s32[16,512]{1,0:T(8,128)} %bitcast.7, s32[1,512]{1,0:T(1,128)} %bitcast.9, bf16[512,512]{1,0:T(8,128)(2,1)} %ow.1), custom_call_target="tpu_custom_call" | custom-call | tf_op jit(solution)/shard_map/layer/pallas_call | solution.py:316
  39.2 1.5 %copy.10 = bf16[64,512]{1,0:T(8,128)(2,1)} copy(bf16[64,512]{1,0:T(8,128)(2,1)} %layer.1) | data formatting | bytes 131072

commit v4 on v3

--- a/solution.py
+++ b/solution.py
@@ -20,10 +20,10 @@
     return RING[k // 8] + RING[(k // 2) % 4]
 
 
-FAR = sorted((k for k in range(1, OWNERS) if hops(k) >= 2), key=lambda k: -hops(k))
+FAR = sorted((k for k in range(1, OWNERS) if hops(k) >= 2), key=lambda k: -hops(k))[::-1]
 NEAR = [2, 6, 8, 24, 3, 7, 9, 25, 1]
 PEERS = FAR + NEAR
-HELD = 6
+HELD = 0
 
 
 def shifted(k, sign):
@@ -174,19 +174,21 @@
         copy.start()
         sends.append(copy)
 
-    for n, k in enumerate(PEERS):
-        count = HALF if k in FAR else CAP
-        for part in range(count // HALF):
+    def serve(k):
+        parts = 1 if k in FAR else 2
+        for part in range(parts):
             ask(k, part, 0, shifted(k, 1)).wait_recv()
 
-        def some(part, carry, k=k):
+        def some(part, carry):
             pick(feat, lambda u: req_sm[k, part, u], stage, 0, HALF)
             sendbuf[k, part] = pack(stage[...]).astype(jnp.bfloat16)
             return carry
 
-        lax.fori_loop(0, count // HALF, some, 0)
-        if 1 <= n <= len(FAR):
-            send(PEERS[n - 1])
+        lax.fori_loop(0, parts, some, 0)
+        send(k)
+
+    for k in FAR:
+        serve(k)
 
     def spread(k, part):
         place = pl.multiple_of(shifted(k, -1) * CAP + part * HALF, HALF)
@@ -209,7 +211,7 @@
             along.append(copy)
         spread(k, half)
         if HELD <= n < HELD + len(NEAR):
-            send(NEAR[n - HELD])
+            serve(NEAR[n - HELD])
     for z in range(1, HEADS):
         other = (h + HEADS - z) % HEADS
         pltpu.make_async_remote_copy(

time: 40.8 us -> 39.3 us (0.963)
  Pallas kernels: 39.2 us -> 37.7 us
    pallas_call x1, Pallas kernels: 39.2 us -> 37.7 us  [local(): pl.pallas_call(kernel, out_shape=jax.ShapeDtypeStruct((ROWS, OUT), jnp.bf...]
where the time goes in v4:
time: 39.3 us; the launch traced here: 39.2 us
  Pallas kernels  37.7 us (96%)
  local copies, waits for them, and re-layouts  1.47 us (4%)
    pallas_call x1, Pallas kernels, local(): pl.pallas_call(kernel, out_shape=jax.ShapeDtypeStruct((ROWS, OUT), jnp.bf...  37.7 us
    unnamed x1, local copies, waits for them, and re-layouts  1.47 us

profile of v4, /device:TPU:1, one launch (start us, length us, event | category | flops | bytes accessed | tf_op | source)
XLA Modules:
  0.0 39.2 jit_solution(5926697152533754302)
XLA Ops:
  0.0 37.7 %layer.1 = bf16[64,512]{1,0:T(8,128)(2,1)} custom-call(bf16[100,2048]{1,0:T(8,128)(2,1)} %bitcast.5, bf16[64,100]{1,0:T(8,128)(2,1)} %bitcast.8, f32[1,64]{1,0:T(1,128)} %s_src.1, f32[1,64]{1,0:T(1,128)} %s_dst.1, s32[32,256]{1,0:T(8,128)} %bitcast.6, s32[16,512]{1,0:T(8,128)} %bitcast.7, s32[1,512]{1,0:T(1,128)} %bitcast.9, bf16[512,512]{1,0:T(8,128)(2,1)} %ow.1), custom_call_target="tpu_custom_call" | custom-call | tf_op jit(solution)/shard_map/layer/pallas_call | solution.py:318
  37.7 1.5 %copy.10 = bf16[64,512]{1,0:T(8,128)(2,1)} copy(bf16[64,512]{1,0:T(8,128)(2,1)} %layer.1) | data formatting | bytes 131072

commit v5 on v4

--- a/solution.py
+++ b/solution.py
@@ -20,7 +20,7 @@
     return RING[k // 8] + RING[(k // 2) % 4]
 
 
-FAR = sorted((k for k in range(1, OWNERS) if hops(k) >= 2), key=lambda k: -hops(k))[::-1]
+FAR = sorted((k for k in range(1, OWNERS) if hops(k) >= 2), key=lambda k: (hops(k), -(k % 2), -k))
 NEAR = [2, 6, 8, 24, 3, 7, 9, 25, 1]
 PEERS = FAR + NEAR
 HELD = 0
@@ -247,6 +247,8 @@
             return carry
 
         lax.fori_loop(0, 2, both_halves, 0)
+    for copy in sends + along:
+        copy.wait_send()
     for k in FAR:
         hand(k, down, 1 - half, 0).wait_recv()
         hand(k, up, 1 - half, 1).wait_recv()
@@ -304,9 +306,6 @@
     hidden = hidden.T[0:ROWS, :].astype(jnp.bfloat16)
     ow_load.wait()
     out[...] = jnp.dot(hidden, ow_in[...], preferred_element_type=jnp.float32).astype(jnp.bfloat16)
-
-    for copy in sends + along:
-        copy.wait_send()
 
 
 def local(

time: 39.3 us -> 38.7 us (0.985)
  Pallas kernels: 37.7 us -> 37 us
    pallas_call x1, Pallas kernels: 37.7 us -> 37 us  [local(): pl.pallas_call(kernel, out_shape=jax.ShapeDtypeStruct((ROWS, OUT), jnp.bf...]
where the time goes in v5:
time: 38.7 us; the launch traced here: 38.5 us
  Pallas kernels  37 us (96%)
  local copies, waits for them, and re-layouts  1.47 us (4%)
    pallas_call x1, Pallas kernels, local(): pl.pallas_call(kernel, out_shape=jax.ShapeDtypeStruct((ROWS, OUT), jnp.bf...  37 us
    unnamed x1, local copies, waits for them, and re-layouts  1.47 us

profile of v5, /device:TPU:1, one launch (start us, length us, event | category | flops | bytes accessed | tf_op | source)
XLA Modules:
  0.0 38.5 jit_solution(15549810469628135886)
XLA Ops:
  0.0 37.0 %layer.1 = bf16[64,512]{1,0:T(8,128)(2,1)} custom-call(bf16[100,2048]{1,0:T(8,128)(2,1)} %bitcast.5, bf16[64,100]{1,0:T(8,128)(2,1)} %bitcast.8, f32[1,64]{1,0:T(1,128)} %s_src.1, f32[1,64]{1,0:T(1,128)} %s_dst.1, s32[32,256]{1,0:T(8,128)} %bitcast.6, s32[16,512]{1,0:T(8,128)} %bitcast.7, s32[1,512]{1,0:T(1,128)} %bitcast.9, bf16[512,512]{1,0:T(8,128)(2,1)} %ow.1), custom_call_target="tpu_custom_call" | custom-call | tf_op jit(solution)/shard_map/layer/pallas_call | solution.py:317
  37.1 1.5 %copy.10 = bf16[64,512]{1,0:T(8,128)(2,1)} copy(bf16[64,512]{1,0:T(8,128)(2,1)} %layer.1) | data formatting | bytes 131072

commit v6 on v5

--- a/solution.py
+++ b/solution.py
@@ -187,6 +187,7 @@
         lax.fori_loop(0, parts, some, 0)
         send(k)
 
+    serve(NEAR[-1])
     for k in FAR:
         serve(k)
 
@@ -210,7 +211,7 @@
             copy.start()
             along.append(copy)
         spread(k, half)
-        if HELD <= n < HELD + len(NEAR):
+        if HELD <= n < HELD + len(NEAR) - 1:
             serve(NEAR[n - HELD])
     for z in range(1, HEADS):
         other = (h + HEADS - z) % HEADS

time: 38.7 us -> 38.7 us (level)
  no operation moved by 1% of the time
where the time goes in v6:
time: 38.7 us; the launch traced here: 38.5 us
  Pallas kernels  37 us (96%)
  local copies, waits for them, and re-layouts  1.47 us (4%)
    pallas_call x1, Pallas kernels, local(): pl.pallas_call(kernel, out_shape=jax.ShapeDtypeStruct((ROWS, OUT), jnp.bf...  37 us
    unnamed x1, local copies, waits for them, and re-layouts  1.47 us

profile of v6, /device:TPU:1, one launch (start us, length us, event | category | flops | bytes accessed | tf_op | source)
XLA Modules:
  0.0 38.5 jit_solution(13199333322812616241)
XLA Ops:
  0.0 37.0 %layer.1 = bf16[64,512]{1,0:T(8,128)(2,1)} custom-call(bf16[100,2048]{1,0:T(8,128)(2,1)} %bitcast.5, bf16[64,100]{1,0:T(8,128)(2,1)} %bitcast.8, f32[1,64]{1,0:T(1,128)} %s_src.1, f32[1,64]{1,0:T(1,128)} %s_dst.1, s32[32,256]{1,0:T(8,128)} %bitcast.6, s32[16,512]{1,0:T(8,128)} %bitcast.7, s32[1,512]{1,0:T(1,128)} %bitcast.9, bf16[512,512]{1,0:T(8,128)(2,1)} %ow.1), custom_call_target="tpu_custom_call" | custom-call | tf_op jit(solution)/shard_map/layer/pallas_call | solution.py:318
  37.1 1.5 %copy.10 = bf16[64,512]{1,0:T(8,128)(2,1)} copy(bf16[64,512]{1,0:T(8,128)(2,1)} %layer.1) | data formatting | bytes 131072
